TPU v7x, 512 devices: a whole 4x8x8 slice. The times are simulated.
512 devices in a mesh: tp: 16 (over z, core), ep: 32 (over y, x).
Axes of the slice: x: 4, y: 8, z: 8, core: 2. Of those that a mesh axis runs over, the one named last changes fastest.
Arguments:
- tokens: bfloat16 [12288, 2048], P('ep', 'tp'), may hold values from -6 to 6
- norm_gain: float32 [2048], replicated, may hold values from 0.25 to 1.75
- shared_gate: bfloat16 [2048, 2816], P('ep', 'tp'), may hold values from -0.125 to 0.125
- shared_up: bfloat16 [2048, 2816], P('ep', 'tp'), may hold values from -0.125 to 0.125
- shared_down: bfloat16 [2816, 2048], P('tp', 'ep'), may hold values from -0.21875 to 0.21875
- expert_gate: bfloat16 [16, 32, 176, 2048], P('tp', 'ep'), may hold values from -0.125 to 0.125
- expert_up: bfloat16 [16, 32, 176, 2048], P('tp', 'ep'), may hold values from -0.125 to 0.125
- expert_down: bfloat16 [64, 1408, 2048], P('ep', None, 'tp'), may hold values from -0.15625 to 0.15625
- chosen: int32 [64, 384], P('ep'), may hold values from 0 to 12287, as said below
- gates: float32 [64, 384], P('ep'), may hold values from 0.1 to 1
Outputs:
- mixed: bfloat16 [12288, 2048], P('ep', 'tp')
Inputs may be any that keep to these rules, and one draw needn't show every extreme that they name: Each row of chosen holds 384 different token indices in rising order. Of one row, at most 24 lie among the 384 tokens of one index of ep (tokens s * 384 to (s + 1) * 384 - 1), and in every row exactly 24 lie among those of some index.
All inputs are finite; a program needn't handle non-finite values.
Results may differ from a plain program's by a relative error of at most 0.012.
Values may be sent and summed in bfloat16 or wider, within the bound.
A program may use at most 64 MiB of HBM per device.

v0:
```python
import jax
import jax.numpy as jnp
from jax import lax
from jax.sharding import PartitionSpec as P

EXP_DEV = 2
TOK_DEV = 384
CAP = 384
norm_eps = 1e-06


def side_by_side(arrays, axis, dim, along):
    both = jnp.concatenate(arrays, axis=along)
    whole, at, gathered = (lax.all_gather(both, axis, axis=dim, tiled=True), 0, [])
    for a in arrays:
        gathered.append(lax.slice_in_dim(whole, at, at + a.shape[along], axis=along))
        at += a.shape[along]
    return tuple(gathered)


def sent_to_all(array, axis):
    length = lax.axis_size(axis)
    return lax.all_to_all(
        jnp.broadcast_to(array[None], (length, *array.shape)), axis, 0, 0, tiled=True
    )


def joined_along(pieces, dim):
    dims = list(pieces.shape[1:])
    dims[dim] *= pieces.shape[0]
    return jnp.moveaxis(pieces, 0, dim).reshape(dims)


def gathered_copies(array, axis, dim):
    pieces = sent_to_all(array, axis)
    return joined_along(pieces, dim)


def on_device(
    tokens,
    norm_gain,
    shared_gate,
    shared_up,
    shared_down,
    expert_gate,
    expert_up,
    expert_down,
    chosen,
    gates,
):
    tp_count = lax.axis_size("tp")
    ep_count = lax.axis_size("ep")
    slice_width = tokens.shape[1]
    whole = lax.all_gather(tokens, "tp", axis=1, tiled=True)
    widened = whole.astype(jnp.float32)
    inv_scale = lax.rsqrt(jnp.mean(widened * widened, axis=1, keepdims=True) + norm_eps)
    normed = (widened * inv_scale * norm_gain).astype(jnp.bfloat16)
    pieces = side_by_side((shared_gate, shared_up), "ep", 0, 1)
    gate_sum = jnp.dot(normed, pieces[0], preferred_element_type=jnp.float32)
    up_sum = jnp.dot(normed, pieces[1], preferred_element_type=jnp.float32)
    shared_hidden = (jax.nn.silu(gate_sum) * up_sum).astype(jnp.bfloat16)
    partial_out = jnp.dot(
        shared_hidden, gathered_copies(shared_down, "ep", 1), preferred_element_type=jnp.float32
    )
    shared_part = lax.psum_scatter(
        partial_out.astype(jnp.bfloat16), "tp", scatter_dimension=1, tiled=True
    ).astype(jnp.float32)
    slot_most = 2 * CAP // ep_count
    slot_count = ep_count * slot_most
    sources = chosen // TOK_DEV
    source_flags = (
        sources[:, :, None] == jnp.arange(ep_count, dtype=jnp.int32)[None, None, :]
    ).astype(jnp.int32)
    counts = jnp.sum(source_flags, axis=1)
    starts = jnp.cumsum(counts, axis=1) - counts
    run_start = jnp.take_along_axis(starts, sources, axis=1)
    slot_index = sources * slot_most + jnp.arange(CAP, dtype=jnp.int32)[None, :] - run_start
    local_ids = chosen - sources * TOK_DEV
    expert_rows = jnp.arange(EXP_DEV, dtype=jnp.int32)[:, None]
    requests = (
        jnp.full((EXP_DEV, slot_count), TOK_DEV, jnp.int32)
        .at[expert_rows, slot_index]
        .set(local_ids)
    )
    requests = requests.reshape(EXP_DEV, ep_count, slot_most)
    asked_ids = lax.all_to_all(requests, "ep", split_axis=1, concat_axis=1, tiled=True)
    clipped = jnp.minimum(asked_ids, TOK_DEV - 1)
    local_expert = lax.axis_index("tp") // (tp_count // EXP_DEV)
    own_requests = lax.dynamic_index_in_dim(clipped, local_expert, 0, keepdims=False)
    outgoing = jnp.take(normed, own_requests.reshape(-1), axis=0).reshape(ep_count, slot_most, -1)
    arrived = lax.all_to_all(outgoing, "ep", split_axis=0, concat_axis=0, tiled=True)
    token_rows = arrived.reshape(slot_count, -1)
    gate_weight = expert_gate.reshape(expert_gate.shape[2], expert_gate.shape[3])
    up_weight = expert_up.reshape(expert_up.shape[2], expert_up.shape[3])
    gate_values = jnp.einsum(
        "hd,rd->hr", gate_weight, token_rows, preferred_element_type=jnp.float32
    )
    up_values = jnp.einsum("hd,rd->hr", up_weight, token_rows, preferred_element_type=jnp.float32)
    part_hidden = (jax.nn.silu(gate_values) * up_values).astype(jnp.bfloat16)
    all_hidden = lax.all_gather(part_hidden, "tp", axis=0, tiled=True)
    width_hidden = expert_down.shape[1]
    placed_rows = []
    for expert_slot in range(EXP_DEV):
        hidden_block = all_hidden[expert_slot * width_hidden : (expert_slot + 1) * width_hidden, :]
        outputs = jnp.einsum(
            "fr,fd->rd", hidden_block, expert_down[expert_slot], preferred_element_type=jnp.float32
        )
        gate_slots = (
            jnp.zeros((slot_count,), jnp.float32)
            .at[slot_index[expert_slot]]
            .set(gates[expert_slot])
        )
        placed = (gate_slots[:, None] * outputs).astype(jnp.bfloat16)
        placed_rows.append(placed)
    stacked = jnp.stack(placed_rows).reshape(EXP_DEV, ep_count, slot_most, slice_width)
    returned = lax.all_to_all(stacked, "ep", split_axis=1, concat_axis=1, tiled=True)
    flat_values = returned.reshape(-1, slice_width)
    flat_ids = asked_ids.reshape(-1)
    picker = (jnp.arange(TOK_DEV, dtype=jnp.int32)[:, None] == flat_ids[None, :]).astype(
        jnp.bfloat16
    )
    routed = jnp.dot(picker, flat_values, preferred_element_type=jnp.float32)
    return (shared_part + routed).astype(jnp.bfloat16)


def solution(mesh):
    return jax.shard_map(
        on_device,
        mesh=mesh,
        in_specs=(
            P("ep", "tp"),
            P(),
            P("ep", "tp"),
            P("ep", "tp"),
            P("tp", "ep"),
            P("tp", "ep", None, None),
            P("tp", "ep", None, None),
            P("ep", None, "tp"),
            P("ep", None),
            P("ep", None),
        ),
        out_specs=P("ep", "tp"),
        check_vma=False,
    )
```

profile of v0, /device:TPU:4, one launch (start us, length us, event | category | flops | bytes accessed | tf_op | source)
XLA Modules:
  0.0 284.9 jit_solution(4781293270764742484)
XLA Ops:
  9.2 6.6 %gather_fusion.1 = s32[768]{0:T(1024)S(1)} fusion(s32[2,32]{1,0:T(2,128)S(1)} %sub.20, s32[768]{0:T(1024)S(1)} %reshape.168), kind=kCustom, calls=%fused_computation.1 | custom fusion | bytes 12288 | tf_op jit(solution)/shard_map/jit(take_along_axis)/gather | solution.py:76
  15.9 36.5 %scatter_fusion = s32[2,768]{1,0:T(2,128)S(1)} fusion(s32[2,768]{1,0:T(2,128)S(1)} %broadcast_in_dim.23, s32[768]{0:T(1024)S(1)} %reshape.174, s32[768]{0:T(1024)S(1)} %reshape.176), kind=kCustom, calls=%fused_computation.2 | custom fusion | bytes 15360 | tf_op jit(solution)/shard_map/scatter | solution.py:83
  53.1 10.2 %all-to-all-start.1 = ((s32[2,32,24]{2,0,1:T(2,128)}), s32[2,32,24]{2,0,1:T(2,128)S(1)}, u32[]{:S(2)}, u32[]{:S(2)}) async-start(s32[2,32,24]{2,0,1:T(2,128)} %copy.21), calls=%async_computation.1 | async-start | bytes 65536 | tf_op jit(solution)/shard_map/all_to_all | solution.py:86
  63.3 7.8 %all-to-all-done.1 = s32[2,32,24]{2,0,1:T(2,128)S(1)} async-done(((s32[2,32,24]{2,0,1:T(2,128)}), s32[2,32,24]{2,0,1:T(2,128)S(1)}, u32[]{:S(2)}, u32[]{:S(2)}) %all-to-all-start.1) | async-done | bytes 6176 | tf_op jit(solution)/shard_map/all_to_all | solution.py:86
  72.6 1.9 fusion
  74.9 4.3 %gather_fusion = bf16[768,2048]{1,0:T(8,128)(2,1)} fusion(bf16[384,2048]{1,0:T(8,128)(2,1)S(1)} %fusion.2, s32[1024]{0:T(1024)S(1)} %pad_clamp_fusion), kind=kCustom, calls=%fused_computation | custom fusion | bytes 6294528 | tf_op jit(solution)/shard_map/jit(_take)/gather | solution.py:90
  79.2 3.9 %broadcast_select_fusion = bf16[32,24,2048]{2,1,0:T(8,128)(2,1)} fusion(bf16[32,24,2048]{2,1,0:T(8,128)(2,1)} %bitcast.63, pred[32,24]{1,0:T(8,128)(4,1)S(1)} %compare_and_fusion), kind=kLoop, calls=%fused_computation.10 | loop fusion | flops 1572864 | bytes 6292224 | tf_op jit(solution)/shard_map/jit(_take)/select_n | solution.py:90
  83.1 6.8 %all-to-all-start.2 = ((bf16[32,24,2048]{2,1,0:T(8,128)(2,1)}), bf16[32,24,2048]{2,1,0:T(8,128)(2,1)}, u32[]{:S(2)}, u32[]{:S(2)}) async-start(bf16[32,24,2048]{2,1,0:T(8,128)(2,1)} %broadcast_select_fusion), calls=%async_computation.2 | async-start | bytes 6291456 | tf_op jit(solution)/shard_map/all_to_all | solution.py:91
  90.8 73.0 %all-to-all-done.2 = bf16[32,24,2048]{2,1,0:T(8,128)(2,1)} async-done(((bf16[32,24,2048]{2,1,0:T(8,128)(2,1)}), bf16[32,24,2048]{2,1,0:T(8,128)(2,1)}, u32[]{:S(2)}, u32[]{:S(2)}) %all-to-all-start.2) | async-done | bytes 3145760 | tf_op jit(solution)/shard_map/all_to_all | solution.py:91
  163.8 3.2 %convolution_bitcast_fusion.1 = f32[176,768]{1,0:T(8,128)S(1)} fusion(bf16[768,2048]{1,0:T(8,128)(2,1)} %bitcast.7, bf16[1,1,176,2048]{3,2,1,0:T(8,128)(2,1)S(1)} %copy-done), kind=kOutput, calls=%fused_computation.19 | convolution fusion | flops 553648128 | bytes 4407296 | tf_op jit(solution)/shard_map/hd,rd->hr/dot_general | solution.py:95
  167.0 3.8 %fusion.9 = bf16[176,768]{1,0:T(8,128)(2,1)} fusion(bf16[768,2048]{1,0:T(8,128)(2,1)} %bitcast.7, bf16[1,1,176,2048]{3,2,1,0:T(8,128)(2,1)S(1)} %copy-done.8, f32[176,768]{1,0:T(8,128)S(1)} %convolution_bitcast_fusion.1), kind=kOutput, calls=%fused_computation.21 | convolution fusion | flops 554459136 | bytes 4677632 | tf_op jit(solution)/shard_map/hd,rd->hr/dot_general | solution.py:98
  172.0 5.5 %all-to-all-start = ((bf16[32,176,64]{1,2,0:T(8,128)(2,1)}), bf16[32,176,64]{1,2,0:T(8,128)(2,1)S(1)}, u32[]{:S(2)}, u32[]{:S(2)}) async-start(bf16[32,176,64]{1,2,0:T(8,128)(2,1)} %broadcast_in_dim.19), calls=%async_computation | async-start | bytes 2097152 | tf_op jit(solution)/shard_map/all_to_all | solution.py:23
  177.5 9.4 %all-gather.6.cloned.1.call-done = bf16[2048,352]{1,0:T(8,128)(2,1)} async-done(((bf16[64,352]{1,0:T(8,128)(2,1)}), bf16[2048,352]{1,0:T(8,128)(2,1)}) %all-gather.6.cloned.1.call-update) | async-done | bytes 1441808 | tf_op jit(solution)/shard_map/all_gather | solution.py:14
  186.9 2.6 fusion.28
  189.5 14.7 %all-to-all-done = bf16[32,176,64]{1,2,0:T(8,128)(2,1)S(1)} async-done(((bf16[32,176,64]{1,2,0:T(8,128)(2,1)}), bf16[32,176,64]{1,2,0:T(8,128)(2,1)S(1)}, u32[]{:S(2)}, u32[]{:S(2)}) %all-to-all-start) | async-done | bytes 720928 | tf_op jit(solution)/shard_map/all_to_all | solution.py:23
  204.2 4.3 %convolution_convert_fusion = bf16[384,2048]{1,0:T(8,128)(2,1)} fusion(bf16[176,2048]{0,1:T(8,128)(2,1)S(1)} %bitcast.65, bf16[384,2048]{1,0:T(8,128)(2,1)S(1)} %fusion.2, bf16[2048,352]{1,0:T(8,128)(2,1)} %all-gather.6.cloned.1.call-done, f32[384,176]{0,1:T(8,128)} %fusion.28), kind=kOutput, calls=%fused_computation.11 | convolution fusion | flops 554840064 | bytes 5185536 | tf_op jit(solution)/shard_map/dot_general | solution.py:62
  208.5 2.7 copy.26
  211.3 3.1 %scatter_custom_fusion.1 = f32[768]{0:T(1024)S(1)} fusion(s32[384]{0:T(512)S(1)} %get-tuple-element.7, f32[384]{0:T(512)S(1)} %get-tuple-element.5, f32[]{:T(128)} %constant.48.clone.1), kind=kCustom, calls=%fused_computation.73 | custom fusion | bytes 3076 | tf_op jit(solution)/shard_map/scatter | solution.py:111
  214.4 2.9 %scatter_custom_fusion.2 = f32[768]{0:T(1024)S(1)} fusion(s32[384]{0:T(512)S(1)} %get-tuple-element.8, f32[384]{0:T(512)S(1)} %get-tuple-element.6, f32[]{:T(128)} %constant.48.clone.1), kind=kCustom, calls=%fused_computation.71 | custom fusion | bytes 3076 | tf_op jit(solution)/shard_map/scatter | solution.py:111
  217.3 16.4 %all-gather.8.cloned.1.call-done = bf16[2816,768]{1,0:T(8,128)(2,1)} async-done(((bf16[176,768]{1,0:T(8,128)(2,1)}), bf16[2816,768]{1,0:T(8,128)(2,1)}) %all-gather.8.cloned.1.call-update) | async-done | bytes 4325392 | tf_op jit(solution)/shard_map/all_gather | solution.py:100
  233.8 2.5 fusion.17
  238.2 9.9 %all-to-all-start.3 = ((bf16[2,32,24,128]{3,2,0,1:T(8,128)(2,1)}), bf16[2,32,24,128]{3,2,0,1:T(8,128)(2,1)S(1)}, u32[]{:S(2)}, u32[]{:S(2)}) async-start(bf16[2,32,24,128]{3,2,0,1:T(8,128)(2,1)} %pad_maximum_fusion), calls=%async_computation.3 | async-start | bytes 786432 | tf_op jit(solution)/shard_map/all_to_all | solution.py:116
  248.2 27.1 %reduce-scatter.4.cloned.1.call-done = bf16[128,384]{1,0:T(8,128)(2,1)} async-done(((bf16[2048,384]{1,0:T(8,128)(2,1)}), bf16[128,384]{1,0:T(8,128)(2,1)}) %reduce-scatter.4.cloned.1.call-update) | async-done | bytes 98320
  276.3 1.2 fusion.25
  (61 shorter events, 9.4 us)
Async XLA Ops:
  7.4 156.5 %copy-start = (bf16[1,1,176,2048]{3,2,1,0:T(8,128)(2,1)S(1)}, bf16[1,1,176,2048]{3,2,1,0:T(8,128)(2,1)}, u32[]{:S(2)}) copy-start(bf16[1,1,176,2048]{3,2,1,0:T(8,128)(2,1)} %param.15) | copy-start | bytes 2162692
  7.4 65.2 %all-gather.4.cloned.1.call-start = ((), (), s32[]{:S(2)}) async-start(), calls=%async_computation.5 | async-start | bytes 1671168 | tf_op jit(solution)/shard_map/all_gather | solution.py:54
  15.8 58.6 %copy-start.5 = (f32[2048]{0:T(1024)S(1)}, f32[2048]{0:T(1024)}, u32[]{:S(2)}) copy-start(f32[2048]{0:T(1024)} %param.11) | copy-start | bytes 24580
  53.1 18.1 %all-to-all-start.1 = ((s32[2,32,24]{2,0,1:T(2,128)}), s32[2,32,24]{2,0,1:T(2,128)S(1)}, u32[]{:S(2)}, u32[]{:S(2)}) async-start(s32[2,32,24]{2,0,1:T(2,128)} %copy.21), calls=%async_computation.1 | async-start | bytes 65536 | tf_op jit(solution)/shard_map/all_to_all | solution.py:86
  72.6 1.9 copy-start.1
  83.1 6.9 %copy-start.2 = (bf16[64,176]{1,0:T(8,128)(2,1)S(1)}, bf16[64,176]{1,0:T(8,128)(2,1)}, u32[]{:S(2)}) copy-start(bf16[64,176]{1,0:T(8,128)(2,1)} %param.13) | copy-start | bytes 67588
  83.1 6.9 %copy-start.3 = (bf16[64,176]{1,0:T(8,128)(2,1)S(1)}, bf16[64,176]{1,0:T(8,128)(2,1)}, u32[]{:S(2)}) copy-start(bf16[64,176]{1,0:T(8,128)(2,1)} %param.12) | copy-start | bytes 67588
  83.1 80.7 %all-to-all-start.2 = ((bf16[32,24,2048]{2,1,0:T(8,128)(2,1)}), bf16[32,24,2048]{2,1,0:T(8,128)(2,1)}, u32[]{:S(2)}, u32[]{:S(2)}) async-start(bf16[32,24,2048]{2,1,0:T(8,128)(2,1)} %broadcast_select_fusion), calls=%async_computation.2 | async-start | bytes 6291456 | tf_op jit(solution)/shard_map/all_to_all | solution.py:91
  89.9 97.0 %all-gather.6.cloned.1.call-start = ((), (), s32[]{:S(2)}) async-start(), calls=%async_computation.6 | async-start | bytes 1622016 | tf_op jit(solution)/shard_map/all_gather | solution.py:14
  90.7 143.0 %all-gather.8.cloned.1.call-start = ((), (), s32[]{:S(2)}) async-start(), calls=%async_computation.7 | async-start | bytes 4595712 | tf_op jit(solution)/shard_map/all_gather | solution.py:100
  163.8 3.2 %copy-start.8 = (bf16[1,1,176,2048]{3,2,1,0:T(8,128)(2,1)S(1)}, bf16[1,1,176,2048]{3,2,1,0:T(8,128)(2,1)}, u32[]{:S(2)}) copy-start(bf16[1,1,176,2048]{3,2,1,0:T(8,128)(2,1)} %param.16) | copy-start | bytes 2162692
  167.0 3.8 %copy-start.4 = (bf16[176,64]{0,1:T(8,128)(2,1)S(1)}, bf16[176,64]{0,1:T(8,128)(2,1)}, u32[]{:S(2)}) copy-start(bf16[176,64]{0,1:T(8,128)(2,1)} %param.14) | copy-start | bytes 67588
  172.0 32.2 %all-to-all-start = ((bf16[32,176,64]{1,2,0:T(8,128)(2,1)}), bf16[32,176,64]{1,2,0:T(8,128)(2,1)S(1)}, u32[]{:S(2)}, u32[]{:S(2)}) async-start(bf16[32,176,64]{1,2,0:T(8,128)(2,1)} %broadcast_in_dim.19), calls=%async_computation | async-start | bytes 2097152 | tf_op jit(solution)/shard_map/all_to_all | solution.py:23
  177.5 97.8 %reduce-scatter.4.cloned.1.call-start = ((), (), s32[]{:S(2)}) async-start(), calls=%async_computation.8 | async-start | bytes 1671168
  208.5 2.7 copy-start.6
  208.5 25.3 %copy-start.9 = (bf16[2,1408,128]{2,1,0:T(8,128)(2,1)S(1)}, bf16[2,1408,128]{2,1,0:T(8,128)(2,1)}, u32[]{:S(2)}) copy-start(bf16[2,1408,128]{2,1,0:T(8,128)(2,1)} %param.17) | copy-start | bytes 2162692
  233.8 2.9 %copy-start.7 = (bf16[2816,768]{1,0:T(8,128)(2,1)S(1)}, bf16[2816,768]{1,0:T(8,128)(2,1)}, u32[]{:S(2)}) copy-start(bf16[2816,768]{1,0:T(8,128)(2,1)} %all-gather.8.cloned.1.call-done) | copy-start | bytes 12976132
  238.2 38.1 %all-to-all-start.3 = ((bf16[2,32,24,128]{3,2,0,1:T(8,128)(2,1)}), bf16[2,32,24,128]{3,2,0,1:T(8,128)(2,1)S(1)}, u32[]{:S(2)}, u32[]{:S(2)}) async-start(bf16[2,32,24,128]{3,2,0,1:T(8,128)(2,1)} %pad_maximum_fusion), calls=%async_computation.3 | async-start | bytes 786432 | tf_op jit(solution)/shard_map/all_to_all | solution.py:116
Sparse Core Ops, SparseCore 0:
  10.2 46.8 all-gather.3
  211.4 63.8 reduce-scatter.3
Sparse Core Ops, SparseCore 1:
  93.6 93.3 all-gather.5
  188.9 44.8 all-gather.7
where the time goes:
time: 286 us; the launch traced here: 285 us
  waiting for transfers between devices  149 us (52%)
  local copies, waits for them, and re-layouts  60.1 us (21%)
  starting transfers between devices  32.5 us (11%)
  matrix products  18.4 us (6%)
  between operations  15.2 us (5%)
  other arithmetic  9.57 us (3%)
    all_to_all x1, waiting for transfers between devices, on_device(): lax.all_to_all(outgoing, 'ep', split_axis=0, concat_axis=0, tiled=True)  73 us
    scatter x1, local copies, waits for them, and re-layouts, on_device(): requests = jnp.full((EXP_DEV, slot_count), TOK_DEV, jnp.int32).at[expert_...  36.5 us
    unnamed x5, waiting for transfers between devices  27.8 us
    all_gather x1, waiting for transfers between devices, on_device(): all_hidden = lax.all_gather(part_hidden, 'tp', axis=0, tiled=True)  16.4 us
    all_to_all x1, waiting for transfers between devices, sent_to_all(): lax.all_to_all(jnp.broadcast_to(array[None], (length, *array.shape)), axi...  14.7 us
    all_to_all x1, starting transfers between devices, on_device(): lax.all_to_all(requests, 'ep', split_axis=1, concat_axis=1, tiled=True)  10.2 us
    all_to_all x1, starting transfers between devices, on_device(): lax.all_to_all(stacked, 'ep', split_axis=1, concat_axis=1, tiled=True)  9.87 us
    all_gather x1, waiting for transfers between devices, side_by_side(): lax.all_gather(both, axis, axis=dim, tiled=True)  9.39 us
  transfers between devices with their start and end apart: 8, of which 6 were waited for; matrix products, arithmetic and copies ran while one was open for 27% of the time, Pallas kernels for 0%

commit v1 on v0

--- a/solution.py
+++ b/solution.py
@@ -97,7 +97,9 @@
     )
     up_values = jnp.einsum("hd,rd->hr", up_weight, token_rows, preferred_element_type=jnp.float32)
     part_hidden = (jax.nn.silu(gate_values) * up_values).astype(jnp.bfloat16)
-    all_hidden = lax.all_gather(part_hidden, "tp", axis=0, tiled=True)
+    all_hidden = jnp.concatenate(
+        lax.all_to_all(jnp.stack([part_hidden] * lax.axis_size("tp")), "tp", 0, 0), axis=0
+    )
     width_hidden = expert_down.shape[1]
     placed_rows = []
     for expert_slot in range(EXP_DEV):

time: 286 us -> 369 us (1.29)
  the two profiles are of different devices: /device:TPU:4 before, /device:TPU:2 now
where the time goes in v1:
time: 369 us
  waiting for transfers between devices  154 us (42%)
  blocking collectives  76.7 us (21%)
  local copies, waits for them, and re-layouts  65.4 us (18%)
  starting transfers between devices  34.1 us (9%)
  between operations  15.2 us (4%)
  matrix products  14.8 us (4%)
  other arithmetic  7.88 us (2%)
    all_gather x1, waiting for transfers between devices, side_by_side(): lax.all_gather(both, axis, axis=dim, tiled=True)  80.4 us
    all_to_all x1, blocking collectives, on_device(): lax.all_to_all(outgoing, 'ep', split_axis=0, concat_axis=0, tiled=True)  76.7 us
    unnamed x4, waiting for transfers between devices  43.8 us
    scatter x1, local copies, waits for them, and re-layouts, on_device(): requests = jnp.full((EXP_DEV, slot_count), TOK_DEV, jnp.int32).at[expert_...  36.5 us
    all_to_all x1, waiting for transfers between devices, sent_to_all(): lax.all_to_all(jnp.broadcast_to(array[None], (length, *array.shape)), axi...  21.3 us
    all_to_all x1, starting transfers between devices, on_device(): lax.all_to_all(jnp.stack([part_hidden] * lax.axis_size('tp')), 'tp', 0, 0)  10.6 us
    all_to_all x1, starting transfers between devices, on_device(): lax.all_to_all(requests, 'ep', split_axis=1, concat_axis=1, tiled=True)  10.3 us
    all_to_all x1, waiting for transfers between devices, on_device(): lax.all_to_all(requests, 'ep', split_axis=1, concat_axis=1, tiled=True)  8.62 us
  transfers between devices with their start and end apart: 7, of which 5 were waited for; matrix products, arithmetic and copies ran while one was open for 20% of the time, Pallas kernels for 0%

profile of v1, /device:TPU:2, one launch (start us, length us, event | category | flops | bytes accessed | tf_op | source)
XLA Modules:
  0.0 368.6 jit_solution(2428803066650699998)
XLA Ops:
  9.2 6.6 %gather_fusion.1 = s32[768]{0:T(1024)S(1)} fusion(s32[2,32]{1,0:T(2,128)S(1)} %sub.20, s32[768]{0:T(1024)S(1)} %reshape.173), kind=kCustom, calls=%fused_computation.1 | custom fusion | bytes 12288 | tf_op jit(solution)/shard_map/jit(take_along_axis)/gather | solution.py:76
  15.9 36.5 %scatter_fusion = s32[2,768]{1,0:T(2,128)S(1)} fusion(s32[2,768]{1,0:T(2,128)S(1)} %broadcast_in_dim.23, s32[768]{0:T(1024)S(1)} %reshape.179, s32[768]{0:T(1024)S(1)} %reshape.181), kind=kCustom, calls=%fused_computation.2 | custom fusion | bytes 15360 | tf_op jit(solution)/shard_map/scatter | solution.py:83
  53.1 10.3 %all-to-all-start.1 = ((s32[2,32,24]{2,0,1:T(2,128)}), s32[2,32,24]{2,0,1:T(2,128)S(1)}, u32[]{:S(2)}, u32[]{:S(2)}) async-start(s32[2,32,24]{2,0,1:T(2,128)} %copy.21), calls=%async_computation.1 | async-start | bytes 65536 | tf_op jit(solution)/shard_map/all_to_all | solution.py:86
  63.4 8.6 %all-to-all-done.1 = s32[2,32,24]{2,0,1:T(2,128)S(1)} async-done(((s32[2,32,24]{2,0,1:T(2,128)}), s32[2,32,24]{2,0,1:T(2,128)S(1)}, u32[]{:S(2)}, u32[]{:S(2)}) %all-to-all-start.1) | async-done | bytes 6176 | tf_op jit(solution)/shard_map/all_to_all | solution.py:86
  73.4 1.9 fusion
  75.8 4.3 %gather_fusion = bf16[768,2048]{1,0:T(8,128)(2,1)} fusion(bf16[384,2048]{1,0:T(8,128)(2,1)S(1)} %fusion.2, s32[1024]{0:T(1024)S(1)} %pad_clamp_fusion), kind=kCustom, calls=%fused_computation | custom fusion | bytes 6294528 | tf_op jit(solution)/shard_map/jit(_take)/gather | solution.py:90
  80.0 2.2 broadcast_select_fusion
  82.3 76.7 %all_to_all.25 = bf16[32,24,2048]{2,1,0:T(8,128)(2,1)} all-to-all(bf16[32,24,2048]{2,1,0:T(8,128)(2,1)S(1)} %broadcast_select_fusion), channel_id=1, replica_groups=mesh['tp'=16,'ep'=32] {'ep'}, dimensions={0} | all-to-all | bytes 6291456 | tf_op jit(solution)/shard_map/all_to_all | solution.py:91
  160.1 5.6 %all-to-all-start = ((bf16[32,176,64]{1,2,0:T(8,128)(2,1)}), bf16[32,176,64]{1,2,0:T(8,128)(2,1)S(1)}, u32[]{:S(2)}, u32[]{:S(2)}) async-start(bf16[32,176,64]{1,2,0:T(8,128)(2,1)} %broadcast_in_dim.19), calls=%async_computation | async-start | bytes 2097152 | tf_op jit(solution)/shard_map/all_to_all | solution.py:23
  165.7 3.2 convolution_bitcast_fusion.1
  169.0 1.9 fusion.5
  170.9 21.3 %all-to-all-done = bf16[32,176,64]{1,2,0:T(8,128)(2,1)S(1)} async-done(((bf16[32,176,64]{1,2,0:T(8,128)(2,1)}), bf16[32,176,64]{1,2,0:T(8,128)(2,1)S(1)}, u32[]{:S(2)}, u32[]{:S(2)}) %all-to-all-start) | async-done | bytes 720928 | tf_op jit(solution)/shard_map/all_to_all | solution.py:23
  192.2 3.2 stack.8
  195.4 10.6 %all-to-all-start.3 = ((bf16[16,176,768]{2,1,0:T(8,128)(2,1)}), bf16[16,176,768]{2,1,0:T(8,128)(2,1)}, u32[]{:S(2)}, u32[]{:S(2)}) async-start(bf16[16,176,768]{2,1,0:T(8,128)(2,1)} %stack.8), calls=%async_computation.3 | async-start | bytes 8650752 | tf_op jit(solution)/shard_map/all_to_all | solution.py:101
  206.9 80.4 %all-gather.5.cloned.1.call-done = bf16[2048,352]{1,0:T(8,128)(2,1)} async-done(((bf16[64,352]{1,0:T(8,128)(2,1)}), bf16[2048,352]{1,0:T(8,128)(2,1)}) %all-gather.5.cloned.1.call-update) | async-done | bytes 1441808 | tf_op jit(solution)/shard_map/all_gather | solution.py:14
  287.3 2.6 fusion.14
  289.9 4.3 %convolution_convert_fusion = bf16[384,2048]{1,0:T(8,128)(2,1)} fusion(bf16[176,2048]{0,1:T(8,128)(2,1)S(1)} %bitcast.73, bf16[384,2048]{1,0:T(8,128)(2,1)S(1)} %fusion.2, bf16[2048,352]{1,0:T(8,128)(2,1)} %all-gather.5.cloned.1.call-done, f32[384,176]{0,1:T(8,128)} %fusion.14), kind=kOutput, calls=%fused_computation.11 | convolution fusion | flops 554840064 | bytes 5185536 | tf_op jit(solution)/shard_map/dot_general | solution.py:62
  294.2 2.6 copy.26
  296.9 3.1 scatter_custom_fusion.1
  300.0 2.9 scatter_custom_fusion.2
  303.2 2.5 fusion.43
  308.1 7.6 %all-to-all-start.4 = ((bf16[2,32,24,128]{3,2,0,1:T(8,128)(2,1)}), bf16[2,32,24,128]{3,2,0,1:T(8,128)(2,1)S(1)}, u32[]{:S(2)}, u32[]{:S(2)}) async-start(bf16[2,32,24,128]{3,2,0,1:T(8,128)(2,1)} %pad_maximum_fusion), calls=%async_computation.4 | async-start | bytes 786432 | tf_op jit(solution)/shard_map/all_to_all | solution.py:118
  315.8 43.1 %reduce-scatter.4.cloned.1.call-done = bf16[128,384]{1,0:T(8,128)(2,1)} async-done(((bf16[2048,384]{1,0:T(8,128)(2,1)}), bf16[128,384]{1,0:T(8,128)(2,1)}) %reduce-scatter.4.cloned.1.call-update) | async-done | bytes 98320
  360.0 1.2 fusion.11
  (61 shorter events, 10.0 us)
Async XLA Ops:
  7.4 158.3 %copy-start = (bf16[1,1,176,2048]{3,2,1,0:T(8,128)(2,1)S(1)}, bf16[1,1,176,2048]{3,2,1,0:T(8,128)(2,1)}, u32[]{:S(2)}) copy-start(bf16[1,1,176,2048]{3,2,1,0:T(8,128)(2,1)} %param.15) | copy-start | bytes 2162692
  7.4 66.0 %all-gather.3.cloned.1.call-start = ((), (), s32[]{:S(2)}) async-start(), calls=%async_computation.6 | async-start | bytes 1671168 | tf_op jit(solution)/shard_map/all_gather | solution.py:54
  15.8 59.5 %copy-start.6 = (f32[2048]{0:T(1024)S(1)}, f32[2048]{0:T(1024)}, u32[]{:S(2)}) copy-start(f32[2048]{0:T(1024)} %param.11) | copy-start | bytes 24580
  53.1 18.9 %all-to-all-start.1 = ((s32[2,32,24]{2,0,1:T(2,128)}), s32[2,32,24]{2,0,1:T(2,128)S(1)}, u32[]{:S(2)}, u32[]{:S(2)}) async-start(s32[2,32,24]{2,0,1:T(2,128)} %copy.21), calls=%async_computation.1 | async-start | bytes 65536 | tf_op jit(solution)/shard_map/all_to_all | solution.py:86
  73.4 1.9 copy-start.1
  82.3 76.7 %copy-start.3 = (bf16[176,64]{0,1:T(8,128)(2,1)S(1)}, bf16[176,64]{0,1:T(8,128)(2,1)}, u32[]{:S(2)}) copy-start(bf16[176,64]{0,1:T(8,128)(2,1)} %param.14) | copy-start | bytes 67588
  160.1 32.1 %all-to-all-start = ((bf16[32,176,64]{1,2,0:T(8,128)(2,1)}), bf16[32,176,64]{1,2,0:T(8,128)(2,1)S(1)}, u32[]{:S(2)}, u32[]{:S(2)}) async-start(bf16[32,176,64]{1,2,0:T(8,128)(2,1)} %broadcast_in_dim.19), calls=%async_computation | async-start | bytes 2097152 | tf_op jit(solution)/shard_map/all_to_all | solution.py:23
  165.7 3.3 copy-start.2
  165.7 3.3 copy-start.8
  195.4 10.7 %copy-start.4 = (bf16[64,176]{1,0:T(8,128)(2,1)S(1)}, bf16[64,176]{1,0:T(8,128)(2,1)}, u32[]{:S(2)}) copy-start(bf16[64,176]{1,0:T(8,128)(2,1)} %param.13) | copy-start | bytes 67588
  195.4 10.7 %copy-start.5 = (bf16[64,176]{1,0:T(8,128)(2,1)S(1)}, bf16[64,176]{1,0:T(8,128)(2,1)}, u32[]{:S(2)}) copy-start(bf16[64,176]{1,0:T(8,128)(2,1)} %param.12) | copy-start | bytes 67588
  195.4 107.8 %all-to-all-start.3 = ((bf16[16,176,768]{2,1,0:T(8,128)(2,1)}), bf16[16,176,768]{2,1,0:T(8,128)(2,1)}, u32[]{:S(2)}, u32[]{:S(2)}) async-start(bf16[16,176,768]{2,1,0:T(8,128)(2,1)} %stack.8), calls=%async_computation.3 | async-start | bytes 8650752 | tf_op jit(solution)/shard_map/all_to_all | solution.py:101
  206.1 81.3 %all-gather.5.cloned.1.call-start = ((), (), s32[]{:S(2)}) async-start(), calls=%async_computation.7 | async-start | bytes 1622016 | tf_op jit(solution)/shard_map/all_gather | solution.py:14
  206.8 152.0 %reduce-scatter.4.cloned.1.call-start = ((), (), s32[]{:S(2)}) async-start(), calls=%async_computation.8 | async-start | bytes 1671168
  294.2 2.7 copy-start.7
  303.0 2.8 copy-start.9
  308.1 51.8 %all-to-all-start.4 = ((bf16[2,32,24,128]{3,2,0,1:T(8,128)(2,1)}), bf16[2,32,24,128]{3,2,0,1:T(8,128)(2,1)S(1)}, u32[]{:S(2)}, u32[]{:S(2)}) async-start(bf16[2,32,24,128]{3,2,0,1:T(8,128)(2,1)} %pad_maximum_fusion), calls=%async_computation.4 | async-start | bytes 786432 | tf_op jit(solution)/shard_map/all_to_all | solution.py:118
Sparse Core Ops, SparseCore 0:
  10.2 46.8 all-gather.2
  297.0 61.8 reduce-scatter.3
Sparse Core Ops, SparseCore 1:
  209.7 77.6 all-gather.4
